TPU v7x, 32 devices: a whole 2x2x4 slice. The times are simulated.
32 devices in a mesh: gx: 4 (over y, x), gy: 8 (over z, core).
Axes of the slice: x: 2, y: 2, z: 4, core: 2. Of those that a mesh axis runs over, the one named last changes fastest.
Arguments:
- features: bfloat16 [32, 32, 64, 128], P(None, 'gx', 'gy'), may hold values from -6 to 6
- weight_two: bfloat16 [27, 32, 32], replicated, may hold values from -0.21875 to 0.21875
- bias_two: float32 [32], replicated, may hold values from -3 to 3
- weight_three: bfloat16 [27, 64, 32], replicated, may hold values from -0.21875 to 0.21875
- bias_three: float32 [64], replicated, may hold values from -3 to 3
- weight_four: bfloat16 [27, 128, 64], replicated, may hold values from -0.25 to 0.25
- bias_four: float32 [128], replicated, may hold values from -3 to 3
Outputs:
- level_two: bfloat16 [32, 32, 64, 128], P(None, 'gx', 'gy')
- level_three: bfloat16 [64, 16, 32, 64], P(None, 'gx', 'gy')
- bottleneck: bfloat16 [128, 8, 16, 32], P(None, None, None, 'gy')
All inputs are finite; a program needn't handle non-finite values.
Results may differ from a plain program's by a relative error of at most 0.0085.
Values may be sent and summed in bfloat16 or wider, within the bound.
No kernel may reach another device: no remote copies, remote signals or barrier semaphores. Data moves between devices by JAX's collectives and lax.ppermute only.
A program may use at most 64 MiB of HBM per device.

v0:
```python
import jax
import jax.numpy as jnp
from jax import lax
from jax.sharding import PartitionSpec as P


def extended(cells, sides, width):
    for axis, dim in sides:
        count = lax.axis_size(axis)
        head = lax.slice_in_dim(cells, 0, width, axis=dim)
        tail = lax.slice_in_dim(cells, cells.shape[dim] - width, cells.shape[dim], axis=dim)
        cells = jnp.concatenate(
            [
                lax.ppermute(tail, axis, [(i, (i + 1) % count) for i in range(count)]),
                cells,
                lax.ppermute(head, axis, [((i + 1) % count, i) for i in range(count)]),
            ],
            axis=dim,
        )
    return cells


def wrap_axis(source, axis):
    first = lax.slice_in_dim(source, 0, 1, axis=axis)
    final = lax.slice_in_dim(source, source.shape[axis] - 1, source.shape[axis], axis=axis)
    return jnp.concatenate([final, source, first], axis=axis)


def convolve(padded, weights, bias_values):
    in_channels = padded.shape[0]
    extent_x = padded.shape[1] - 2
    extent_y = padded.shape[2] - 2
    extent_z = padded.shape[3] - 2
    out_channels = weights.shape[1]
    running = jnp.zeros((out_channels, extent_x * extent_y * extent_z), jnp.float32)
    for offset_x in range(3):
        for offset_y in range(3):
            stacked = jnp.concatenate(
                [
                    padded[
                        :,
                        offset_x : offset_x + extent_x,
                        offset_y : offset_y + extent_y,
                        offset_z : offset_z + extent_z,
                    ]
                    for offset_z in range(3)
                ],
                axis=0,
            ).reshape(3 * in_channels, -1)
            first_row = offset_x * 9 + offset_y * 3
            mixing = (
                weights[first_row : first_row + 3]
                .transpose(1, 0, 2)
                .reshape(out_channels, 3 * in_channels)
            )
            running = running + jnp.dot(mixing, stacked, preferred_element_type=jnp.float32)
    result = running + bias_values[:, None]
    result = jax.nn.leaky_relu(result, 0.1).astype(jnp.bfloat16)
    return result.reshape(out_channels, extent_x, extent_y, extent_z)


def average_pool(source):
    channels, extent_x, extent_y, extent_z = source.shape
    blocks = source.astype(jnp.float32).reshape(
        channels, extent_x // 2, 2, extent_y // 2, 2, extent_z // 2, 2
    )
    return blocks.mean(axis=(2, 4, 6)).astype(jnp.bfloat16)


def shards(features, weight_two, bias_two, weight_three, bias_three, weight_four, bias_four):
    rimmed = extended(features, (("gx", 1), ("gy", 2)), 1)
    level_two = convolve(wrap_axis(rimmed, 3), weight_two, bias_two)
    pooled = average_pool(level_two)
    rimmed_three = extended(pooled, (("gx", 1), ("gy", 2)), 1)
    level_three = convolve(wrap_axis(rimmed_three, 3), weight_three, bias_three)
    coarse = average_pool(level_three)
    pieces = lax.all_to_all(coarse, "gy", split_axis=3, concat_axis=2, tiled=True)
    slab_rows = lax.all_gather(pieces, "gx", axis=1, tiled=True)
    deepened = extended(slab_rows, (("gy", 3),), 1)
    padded = wrap_axis(wrap_axis(deepened, 1), 2)
    bottleneck = convolve(padded, weight_four, bias_four)
    return (level_two, level_three, bottleneck)


def solution(mesh):
    return jax.shard_map(
        shards,
        mesh=mesh,
        in_specs=(P(None, "gx", "gy", None), P(), P(), P(), P(), P(), P()),
        out_specs=(P(None, "gx", "gy", None), P(None, "gx", "gy", None), P(None, None, None, "gy")),
        check_vma=False,
    )
```

profile of v0, /device:TPU:0, one launch (start us, length us, event | category | flops | bytes accessed | tf_op | source)
XLA Modules:
  0.0 100.0 jit_solution(3070848087950724654)
XLA Ops:
  0.6 1.5 %copy.174 = bf16[32,8,8,128]{3,0,2,1:T(8,128)(2,1)S(1)} copy(bf16[32,8,8,128]{3,2,1,0:T(8,128)(2,1)} %param.7) | data formatting | bytes 1048576 | tf_op args[0]
  2.1 3.0 %collective-permute-start = (bf16[32,1,8,128]{3,0,2,1:T(8,128)(2,1)S(1)}, bf16[32,1,8,128]{3,0,2,1:T(8,128)(2,1)S(1)}, u32[]{:S(2)}, u32[]{:S(2)}) collective-permute-start(bf16[32,1,8,128]{3,0,2,1:T(8,128)(2,1)S(1)} %get-tuple-element.57), channel_id=1, source_target_pairs={{0,8},{8,16},{16,24},{24,0},{1,9},{9,17},{17,25},{25,1},{2,10},{10... | collective-permute-start | bytes 196616 | tf_op jit(solution)/shard_map/ppermute | solution.py:14
  6.2 2.3 %collective-permute-done = bf16[32,1,8,128]{3,0,2,1:T(8,128)(2,1)S(1)} collective-permute-done((bf16[32,1,8,128]{3,0,2,1:T(8,128)(2,1)S(1)}, bf16[32,1,8,128]{3,0,2,1:T(8,128)(2,1)S(1)}, u32[]{:S(2)}, u32[]{:S(2)}) %collective-permute-start) | collective-permute-done | bytes 65568 | tf_op jit(solution)/shard_map/ppermute | solution.py:14
  9.9 2.2 %collective-permute-start.3 = (bf16[32,10,1,128]{3,0,2,1:T(8,128)(2,1)S(1)}, bf16[32,10,1,128]{3,0,2,1:T(8,128)(2,1)S(1)}, u32[]{:S(2)}, u32[]{:S(2)}) collective-permute-start(bf16[32,10,1,128]{3,0,2,1:T(8,128)(2,1)S(1)} %get-tuple-element.52), channel_id=1, source_target_pairs={{1,0},{2,1},{3,2},{4,3},{5,4},{6,5},{7,6},{0,7},{9,8},{10,9},{11,1... | collective-permute-start | bytes 245768 | tf_op jit(solution)/shard_map/ppermute | solution.py:16
  14.2 3.6 %collective-permute-done.2 = bf16[32,10,1,128]{3,0,2,1:T(8,128)(2,1)S(1)} collective-permute-done((bf16[32,10,1,128]{3,0,2,1:T(8,128)(2,1)S(1)}, bf16[32,10,1,128]{3,0,2,1:T(8,128)(2,1)S(1)}, u32[]{:S(2)}, u32[]{:S(2)}) %collective-permute-start.2) | collective-permute-done | bytes 81952 | tf_op jit(solution)/shard_map/ppermute | solution.py:14
  18.2 1.7 %maximum_maximum_fusion = (bf16[32,10,10,129]{3,0,2,1:T(8,128)(2,1)S(1)}, bf16[32,10,10,129]{3,0,2,1:T(8,128)(2,1)S(1)}) fusion(bf16[32,10,1,128]{3,0,2,1:T(8,128)(2,1)S(1)} %collective-permute-done.3, bf16[32,10,8,128]{3,0,2,1:T(8,128)(2,1)S(1)} %constant_dynamic-update-slice_fusion, bf16[32,10,1,128]{3,0,2,1:T(8,128)(2,1)S(1)} %collective-permute-done.2, ...), kind=kLoop, calls=%fused_computation.11 | loop fusion | flops 6604800 | bytes 2483200 | tf_op jit(solution)/shard_map/concatenate | solution.py:26
  19.9 2.8 %fusion.60 = (bf16[32,8,8,128]{3,0,2,1:T(8,128)(2,1)S(1)}, bf16[32,8,8,128]{3,0,2,1:T(8,128)(2,1)S(1)}, bf16[32,8,8,128]{3,0,2,1:T(8,128)(2,1)S(1)}, bf16[32,8,8...) fusion(bf16[32,10,10,129]{3,0,2,1:T(8,128)(2,1)S(1)} %get-tuple, ...), kind=kLoop, calls=%fused_computation.164 | loop fusion | bytes 18874368 | tf_op jit(solution)/shard_map/slice | solution.py:40
  31.1 1.1 %convolution_add_fusion.7 = f32[8192,32]{0,1:T(8,128)S(1)} fusion(f32[8192,32]{0,1:T(8,128)S(1)} %fusion.18, bf16[32,96]{1,0:T(8,128)(2,1)S(1)} %reshape.191, bf16[12,8,64,128]{3,2,1,0:T(8,128)(2,1)S(1)} %bitcast.227), kind=kOutput, calls=%fused_computation.9 | convolution fusion | flops 50593792 | bytes 3676160 | tf_op jit(solution)/shard_map/dot_general | solution.py:56
  33.4 1.1 %convolution_add_fusion.5 = f32[8192,32]{0,1:T(8,128)S(1)} fusion(f32[8192,32]{0,1:T(8,128)S(1)} %convolution_add_fusion.6, bf16[32,96]{1,0:T(8,128)(2,1)S(1)} %reshape.195, bf16[12,8,64,128]{3,2,1,0:T(8,128)(2,1)S(1)} %bitcast.230), kind=kOutput, calls=%fused_computation.7 | convolution fusion | flops 50593792 | bytes 3676160 | tf_op jit(solution)/shard_map/dot_general | solution.py:56
  34.5 1.1 %convolution_add_fusion.4 = f32[8192,32]{0,1:T(8,128)S(1)} fusion(f32[8192,32]{0,1:T(8,128)S(1)} %convolution_add_fusion.5, bf16[32,96]{1,0:T(8,128)(2,1)S(1)} %reshape.197, bf16[12,8,64,128]{3,2,1,0:T(8,128)(2,1)S(1)} %bitcast.229), kind=kOutput, calls=%fused_computation.6 | convolution fusion | flops 50593792 | bytes 3676160 | tf_op jit(solution)/shard_map/dot_general | solution.py:56
  36.7 1.1 %convolution_add_fusion.2 = f32[8192,32]{0,1:T(8,128)S(1)} fusion(f32[8192,32]{0,1:T(8,128)S(1)} %convolution_add_fusion.3, bf16[32,96]{1,0:T(8,128)(2,1)S(1)} %reshape.201, bf16[12,8,64,128]{3,2,1,0:T(8,128)(2,1)S(1)} %bitcast.233), kind=kOutput, calls=%fused_computation.4 | convolution fusion | flops 50593792 | bytes 3676160 | tf_op jit(solution)/shard_map/dot_general | solution.py:56
  37.9 1.1 %convolution_add_fusion.1 = f32[8192,32]{0,1:T(8,128)S(1)} fusion(f32[8192,32]{0,1:T(8,128)S(1)} %convolution_add_fusion.2, bf16[32,96]{1,0:T(8,128)(2,1)S(1)} %reshape.203, bf16[12,8,64,128]{3,2,1,0:T(8,128)(2,1)S(1)} %bitcast.232), kind=kOutput, calls=%fused_computation.3 | convolution fusion | flops 50593792 | bytes 3676160 | tf_op jit(solution)/shard_map/dot_general | solution.py:56
  39.0 1.1 %fusion.31 = bf16[32,8192]{1,0:T(8,128)(2,1)S(1)} fusion(f32[8192,32]{0,1:T(8,128)S(1)} %convolution_add_fusion.1, bf16[32,96]{1,0:T(8,128)(2,1)S(1)} %reshape.205, bf16[12,8,64,128]{3,2,1,0:T(8,128)(2,1)S(1)} %bitcast.234, f32[32]{0:T(128)S(1)} %copy-done.13), kind=kOutput, calls=%fused_computation.49 | convolution fusion | flops 51904512 | bytes 3152000 | tf_op jit(solution)/shard_map/dot_general | solution.py:56
  40.1 2.4 %copy.198 = f32[32,8192]{0,1:T(8,128)} copy(bf16[32,8192]{1,0:T(8,128)(2,1)S(1)} %fusion.31) | data formatting | bytes 1572864 | tf_op jit(solution)/shard_map/convert_element_type | solution.py:64
  42.5 4.8 %reduce_sum.18 = f32[32,4,4,64]{0,3,2,1:T(8,128)S(1)} reduce(f32[32,4,2,4,2,64,2]{0,6,5,4,3,2,1:T(2,128)} %bitcast.225, f32[]{:T(128)} %constant.6.clone.1), dimensions={2,4,6}, to_apply=%region_0.1 | reduce | flops 229376 | bytes 1179652 | tf_op jit(solution)/shard_map/reduce_sum | solution.py:67
  47.4 2.1 %collective-permute-start.5 = (bf16[32,1,4,64]{0,3,2,1:T(8,128)(2,1)S(1)}, bf16[32,1,4,64]{0,3,2,1:T(8,128)(2,1)S(1)}, u32[]{:S(2)}, u32[]{:S(2)}) collective-permute-start(bf16[32,1,4,64]{0,3,2,1:T(8,128)(2,1)S(1)} %get-tuple-element.99), channel_id=1, source_target_pairs={{8,0},{16,8},{24,16},{0,24},{9,1},{17,9},{25,17},{1,25},{10,2},{18... | collective-permute-start | bytes 49160 | tf_op jit(solution)/shard_map/ppermute | solution.py:16
  49.6 2.2 %collective-permute-done.5 = bf16[32,1,4,64]{0,3,2,1:T(8,128)(2,1)S(1)} collective-permute-done((bf16[32,1,4,64]{0,3,2,1:T(8,128)(2,1)S(1)}, bf16[32,1,4,64]{0,3,2,1:T(8,128)(2,1)S(1)}, u32[]{:S(2)}, u32[]{:S(2)}) %collective-permute-start.5) | collective-permute-done | bytes 16416 | tf_op jit(solution)/shard_map/ppermute | solution.py:16
  51.8 2.9 %collective-permute-done.4 = bf16[32,1,4,64]{0,3,2,1:T(8,128)(2,1)S(1)} collective-permute-done((bf16[32,1,4,64]{0,3,2,1:T(8,128)(2,1)S(1)}, bf16[32,1,4,64]{0,3,2,1:T(8,128)(2,1)S(1)}, u32[]{:S(2)}, u32[]{:S(2)}) %collective-permute-start.4) | collective-permute-done | bytes 16416 | tf_op jit(solution)/shard_map/ppermute | solution.py:14
  55.3 2.5 %collective-permute-done.7 = bf16[32,6,1,64]{0,3,2,1:T(8,128)(2,1)S(1)} collective-permute-done((bf16[32,6,1,64]{0,3,2,1:T(8,128)(2,1)S(1)}, bf16[32,6,1,64]{0,3,2,1:T(8,128)(2,1)S(1)}, u32[]{:S(2)}, u32[]{:S(2)}) %collective-permute-start.7) | collective-permute-done | bytes 24608 | tf_op jit(solution)/shard_map/ppermute | solution.py:16
  57.8 2.9 %collective-permute-done.6 = bf16[32,6,1,64]{0,3,2,1:T(8,128)(2,1)S(1)} collective-permute-done((bf16[32,6,1,64]{0,3,2,1:T(8,128)(2,1)S(1)}, bf16[32,6,1,64]{0,3,2,1:T(8,128)(2,1)S(1)}, u32[]{:S(2)}, u32[]{:S(2)}) %collective-permute-start.6) | collective-permute-done | bytes 24608 | tf_op jit(solution)/shard_map/ppermute | solution.py:14
  67.9 8.0 %all_to_all.18 = bf16[8,2,512]{2,1,0:T(2,128)(2,1)S(1)} all-to-all(bf16[8,2,512]{2,1,0:T(2,128)(2,1)S(1)} %reshape.247), channel_id=1, replica_groups=mesh['gx'=4,'gy'=8] {'gy'}, dimensions={0} | all-to-all | bytes 32768 | tf_op jit(solution)/shard_map/all_to_all | solution.py:77
  76.0 8.5 %all_gather.3 = bf16[64,8,16,4]{0,2,3,1:T(8,128)(2,1)S(1)} all-gather(bf16[64,2,16,4]{0,2,3,1:T(8,128)(2,1)S(1)} %bitcast.257), channel_id=1, replica_groups=mesh['gx'=4,'gy'=8] {'gx'}, dimensions={1}, use_global_device_ids=true | all-gather | bytes 81920 | tf_op jit(solution)/shard_map/all_gather | solution.py:78
  87.1 3.5 %collective-permute-start.9 = (bf16[64,8,16,1]{0,2,3,1:T(8,128)(2,1)S(1)}, bf16[64,8,16,1]{0,2,3,1:T(8,128)(2,1)S(1)}, u32[]{:S(2)}, u32[]{:S(2)}) collective-permute-start(bf16[64,8,16,1]{0,2,3,1:T(8,128)(2,1)S(1)} %get-tuple-element.130), channel_id=1, source_target_pairs={{1,0},{2,1},{3,2},{4,3},{5,4},{6,5},{7,6},{0,7},{9,8},{10,9},{11,1... | collective-permute-start | bytes 49160 | tf_op jit(solution)/shard_map/ppermute | solution.py:16
  90.7 1.6 %collective-permute-done.9 = bf16[64,8,16,1]{0,2,3,1:T(8,128)(2,1)S(1)} collective-permute-done((bf16[64,8,16,1]{0,2,3,1:T(8,128)(2,1)S(1)}, bf16[64,8,16,1]{0,2,3,1:T(8,128)(2,1)S(1)}, u32[]{:S(2)}, u32[]{:S(2)}) %collective-permute-start.9) | collective-permute-done | bytes 16416 | tf_op jit(solution)/shard_map/ppermute | solution.py:16
  (164 shorter events, 33.3 us)
Async XLA Ops:
  0.6 7.8 %copy-start = (bf16[32,8,8,128]{3,2,1,0:T(8,128)(2,1)S(1)}, bf16[32,8,8,128]{3,2,1,0:T(8,128)(2,1)}, u32[]{:S(2)}) copy-start(bf16[32,8,8,128]{3,2,1,0:T(8,128)(2,1)} %param.7) | copy-start | bytes 1572868
  0.6 11.5 %copy-start.2 = (bf16[27,32,32]{2,1,0:T(8,128)(2,1)S(1)}, bf16[27,32,32]{2,1,0:T(8,128)(2,1)}, u32[]{:S(2)}) copy-start(bf16[27,32,32]{2,1,0:T(8,128)(2,1)} %param.8) | copy-start | bytes 165892
  2.1 6.3 %collective-permute-start = (bf16[32,1,8,128]{3,0,2,1:T(8,128)(2,1)S(1)}, bf16[32,1,8,128]{3,0,2,1:T(8,128)(2,1)S(1)}, u32[]{:S(2)}, u32[]{:S(2)}) collective-permute-start(bf16[32,1,8,128]{3,0,2,1:T(8,128)(2,1)S(1)} %get-tuple-element.57), channel_id=1, source_target_pairs={{0,8},{8,16},{16,24},{24,0},{1,9},{9,17},{17,25},{25,1},{2,10},{10... | collective-permute-start | bytes 196616 | tf_op jit(solution)/shard_map/ppermute | solution.py:14
  5.1 4.7 %collective-permute-start.1 = (bf16[32,1,8,128]{3,0,2,1:T(8,128)(2,1)S(1)}, bf16[32,1,8,128]{3,0,2,1:T(8,128)(2,1)S(1)}, u32[]{:S(2)}, u32[]{:S(2)}) collective-permute-start(bf16[32,1,8,128]{3,0,2,1:T(8,128)(2,1)S(1)} %get-tuple-element.56), channel_id=1, source_target_pairs={{8,0},{16,8},{24,16},{0,24},{9,1},{17,9},{25,17},{1,25},{10,2},{18... | collective-permute-start | bytes 196616 | tf_op jit(solution)/shard_map/ppermute | solution.py:16
  9.9 4.3 %collective-permute-start.3 = (bf16[32,10,1,128]{3,0,2,1:T(8,128)(2,1)S(1)}, bf16[32,10,1,128]{3,0,2,1:T(8,128)(2,1)S(1)}, u32[]{:S(2)}, u32[]{:S(2)}) collective-permute-start(bf16[32,10,1,128]{3,0,2,1:T(8,128)(2,1)S(1)} %get-tuple-element.52), channel_id=1, source_target_pairs={{1,0},{2,1},{3,2},{4,3},{5,4},{6,5},{7,6},{0,7},{9,8},{10,9},{11,1... | collective-permute-start | bytes 245768 | tf_op jit(solution)/shard_map/ppermute | solution.py:16
  12.1 5.7 %collective-permute-start.2 = (bf16[32,10,1,128]{3,0,2,1:T(8,128)(2,1)S(1)}, bf16[32,10,1,128]{3,0,2,1:T(8,128)(2,1)S(1)}, u32[]{:S(2)}, u32[]{:S(2)}) collective-permute-start(bf16[32,10,1,128]{3,0,2,1:T(8,128)(2,1)S(1)} %get-tuple-element.51), channel_id=1, source_target_pairs={{0,1},{1,2},{2,3},{3,4},{4,5},{5,6},{6,7},{7,0},{8,9},{9,10},{10,1... | collective-permute-start | bytes 245768 | tf_op jit(solution)/shard_map/ppermute | solution.py:14
  37.8 1.1 %copy-start.13 = (f32[32]{0:T(128)S(1)}, f32[32]{0:T(128)}, u32[]{:S(2)}) copy-start(f32[32]{0:T(128)} %param.9) | copy-start | bytes 388
  47.3 7.9 %copy-start.3 = (bf16[27,64,32]{1,2,0:T(8,128)(2,1)S(1)}, bf16[27,64,32]{1,2,0:T(8,128)(2,1)}, u32[]{:S(2)}) copy-start(bf16[27,64,32]{1,2,0:T(8,128)(2,1)} %param.10) | copy-start | bytes 331780
  47.4 4.4 %collective-permute-start.5 = (bf16[32,1,4,64]{0,3,2,1:T(8,128)(2,1)S(1)}, bf16[32,1,4,64]{0,3,2,1:T(8,128)(2,1)S(1)}, u32[]{:S(2)}, u32[]{:S(2)}) collective-permute-start(bf16[32,1,4,64]{0,3,2,1:T(8,128)(2,1)S(1)} %get-tuple-element.99), channel_id=1, source_target_pairs={{8,0},{16,8},{24,16},{0,24},{9,1},{17,9},{25,17},{1,25},{10,2},{18... | collective-permute-start | bytes 49160 | tf_op jit(solution)/shard_map/ppermute | solution.py:16
  49.5 5.2 %collective-permute-start.4 = (bf16[32,1,4,64]{0,3,2,1:T(8,128)(2,1)S(1)}, bf16[32,1,4,64]{0,3,2,1:T(8,128)(2,1)S(1)}, u32[]{:S(2)}, u32[]{:S(2)}) collective-permute-start(bf16[32,1,4,64]{0,3,2,1:T(8,128)(2,1)S(1)} %get-tuple-element.98), channel_id=1, source_target_pairs={{0,8},{8,16},{16,24},{24,0},{1,9},{9,17},{17,25},{25,1},{2,10},{10... | collective-permute-start | bytes 49160 | tf_op jit(solution)/shard_map/ppermute | solution.py:14
  54.7 3.1 %collective-permute-start.7 = (bf16[32,6,1,64]{0,3,2,1:T(8,128)(2,1)S(1)}, bf16[32,6,1,64]{0,3,2,1:T(8,128)(2,1)S(1)}, u32[]{:S(2)}, u32[]{:S(2)}) collective-permute-start(bf16[32,6,1,64]{0,3,2,1:T(8,128)(2,1)S(1)} %get-tuple-element.76), channel_id=1, source_target_pairs={{1,0},{2,1},{3,2},{4,3},{5,4},{6,5},{7,6},{0,7},{9,8},{10,9},{11,1... | collective-permute-start | bytes 73736 | tf_op jit(solution)/shard_map/ppermute | solution.py:16
  54.8 5.9 %collective-permute-start.6 = (bf16[32,6,1,64]{0,3,2,1:T(8,128)(2,1)S(1)}, bf16[32,6,1,64]{0,3,2,1:T(8,128)(2,1)S(1)}, u32[]{:S(2)}, u32[]{:S(2)}) collective-permute-start(bf16[32,6,1,64]{0,3,2,1:T(8,128)(2,1)S(1)} %get-tuple-element.75), channel_id=1, source_target_pairs={{0,1},{1,2},{2,3},{3,4},{4,5},{5,6},{6,7},{7,0},{8,9},{9,10},{10,1... | collective-permute-start | bytes 73736 | tf_op jit(solution)/shard_map/ppermute | solution.py:14
  66.2 0.8 copy-start.11
  67.0 17.6 %copy-start.1 = (bf16[27,128,64]{1,2,0:T(8,128)(2,1)S(1)}, bf16[27,128,64]{1,2,0:T(8,128)(2,1)}, u32[]{:S(2)}) copy-start(bf16[27,128,64]{1,2,0:T(8,128)(2,1)} %param.12) | copy-start | bytes 1327108
  84.5 6.1 %collective-permute-start.8 = (bf16[64,8,16,1]{0,2,3,1:T(8,128)(2,1)S(1)}, bf16[64,8,16,1]{0,2,3,1:T(8,128)(2,1)S(1)}, u32[]{:S(2)}, u32[]{:S(2)}) collective-permute-start(bf16[64,8,16,1]{0,2,3,1:T(8,128)(2,1)S(1)} %get-tuple-element.131), channel_id=1, source_target_pairs={{0,1},{1,2},{2,3},{3,4},{4,5},{5,6},{6,7},{7,0},{8,9},{9,10},{10,1... | collective-permute-start | bytes 49160 | tf_op jit(solution)/shard_map/ppermute | solution.py:14
  87.1 5.1 %collective-permute-start.9 = (bf16[64,8,16,1]{0,2,3,1:T(8,128)(2,1)S(1)}, bf16[64,8,16,1]{0,2,3,1:T(8,128)(2,1)S(1)}, u32[]{:S(2)}, u32[]{:S(2)}) collective-permute-start(bf16[64,8,16,1]{0,2,3,1:T(8,128)(2,1)S(1)} %get-tuple-element.130), channel_id=1, source_target_pairs={{1,0},{2,1},{3,2},{4,3},{5,4},{6,5},{7,6},{0,7},{9,8},{10,9},{11,1... | collective-permute-start | bytes 49160 | tf_op jit(solution)/shard_map/ppermute | solution.py:16
  92.2 0.6 copy-start.9
  94.2 0.9 copy-start.10
  96.3 1.0 copy-start.8
  96.5 1.0 %copy-start.7 = (bf16[3,128,64]{1,2,0:T(8,128)(2,1)S(1)}, bf16[3,128,64]{1,2,0:T(8,128)(2,1)}, u32[]{:S(2)}) copy-start(bf16[3,128,64]{1,2,0:T(8,128)(2,1)} %get-tuple-element.70) | copy-start | bytes 147460
  96.8 0.9 copy-start.6
  97.0 1.0 %copy-start.5 = (bf16[3,128,64]{1,2,0:T(8,128)(2,1)S(1)}, bf16[3,128,64]{1,2,0:T(8,128)(2,1)}, u32[]{:S(2)}) copy-start(bf16[3,128,64]{1,2,0:T(8,128)(2,1)} %get-tuple-element.68) | copy-start | bytes 147460
  97.3 0.9 copy-start.4
  98.2 0.9 copy-start.12
where the time goes:
time: 100 us
  local copies, waits for them, and re-layouts  21.7 us (22%)
  waiting for transfers between devices  19.9 us (20%)
  blocking collectives  16.5 us (16%)
  matrix products  14.8 us (15%)
  other arithmetic  12.9 us (13%)
  starting transfers between devices  12.6 us (13%)
  between operations  1.59 us (2%)
    dot_general x27, matrix products, convolve(): jnp.dot(mixing, stacked, preferred_element_type=jnp.float32)  14.8 us
    ppermute x5, waiting for transfers between devices, extended(): lax.ppermute(tail, axis, [(i, (i + 1) % count) for i in range(count)])  11.6 us
    ppermute x5, starting transfers between devices, extended(): lax.ppermute(head, axis, [((i + 1) % count, i) for i in range(count)])  8.9 us
    all_gather x1, blocking collectives, shards(): slab_rows = lax.all_gather(pieces, 'gx', axis=1, tiled=True)  8.49 us
    ppermute x5, waiting for transfers between devices, extended(): lax.ppermute(head, axis, [((i + 1) % count, i) for i in range(count)])  8.26 us
    all_to_all x1, blocking collectives, shards(): lax.all_to_all(coarse, 'gy', split_axis=3, concat_axis=2, tiled=True)  8.02 us
    concatenate x18, local copies, waits for them, and re-layouts, convolve(): jnp.concatenate([padded[:, offset_x:offset_x + extent_x, offset_y:offset_...  6.73 us
    reduce_sum x2, other arithmetic, average_pool(): return blocks.mean(axis=(2, 4, 6)).astype(jnp.bfloat16)  5.15 us
  transfers between devices with their start and end apart: 10, of which 9 were waited for; matrix products, arithmetic and copies ran while one was open for 4% of the time, Pallas kernels for 0%

commit v1 on v0

--- a/solution.py
+++ b/solution.py
@@ -75,7 +75,12 @@
     level_three = convolve(wrap_axis(rimmed_three, 3), weight_three, bias_three)
     coarse = average_pool(level_three)
     pieces = lax.all_to_all(coarse, "gy", split_axis=3, concat_axis=2, tiled=True)
-    slab_rows = lax.all_gather(pieces, "gx", axis=1, tiled=True)
+    ring = [pieces]
+    for hop in range(3):
+        ring.append(lax.ppermute(ring[-1], "gx", [(dev, (dev + 1) % 4) for dev in range(4)]))
+    slab_rows = jnp.roll(
+        jnp.concatenate(ring[::-1], axis=1), (lax.axis_index("gx") + 1) * ring[0].shape[1], axis=1
+    )
     deepened = extended(slab_rows, (("gy", 3),), 1)
     padded = wrap_axis(wrap_axis(deepened, 1), 2)
     bottleneck = convolve(padded, weight_four, bias_four)

time: 100 us -> 104 us (1.040)
  waiting for transfers between devices: 19.9 us -> 35.7 us
  blocking collectives: 16.5 us -> 8.02 us
  starting transfers between devices: 12.6 us -> 9.78 us
    ppermute x0 -> x3, waiting for transfers between devices: none -> 12.4 us  [shards(): lax.ppermute(ring[-1], 'gx', [(dev, (dev + 1) % 4) for dev in range(4)])]
    all_gather x1 -> x0, blocking collectives: 8.49 us -> none  [shards(): slab_rows = lax.all_gather(pieces, 'gx', axis=1, tiled=True)]
    ppermute x5, waiting for transfers between devices: 11.6 us -> 15.5 us  [extended(): lax.ppermute(tail, axis, [(i, (i + 1) % count) for i in range(count)])]
    ppermute x5, starting transfers between devices: 8.9 us -> 5.43 us  [extended(): lax.ppermute(head, axis, [((i + 1) % count, i) for i in range(count)])]
    slice x7 -> x9, local copies, waits for them, and re-layouts: 4.85 us -> 5 us  [convolve(): padded[:, offset_x:offset_x + extent_x, offset_y:offset_y + extent_y, off...]
    unnamed x36 -> x27, local copies, waits for them, and re-layouts: 3.16 us -> 3.04 us
    concatenate x21 -> x22, other arithmetic: 5 us -> 5.07 us  [convolve(): jnp.concatenate([padded[:, offset_x:offset_x + extent_x, offset_y:offset_...]
    concatenate x5 -> x6, other arithmetic: 2.28 us -> 2.34 us  [wrap_axis(): return jnp.concatenate([final, source, first], axis=axis)]
  transfers between devices with their start and end apart: 10 -> 13, of which waited for: 9 -> 13; matrix products, arithmetic and copies ran while one was open for 4% -> 3% of each run, Pallas kernels for 0% -> 0%
where the time goes in v1:
time: 104 us
  waiting for transfers between devices  35.7 us (34%)
  local copies, waits for them, and re-layouts  21.1 us (20%)
  matrix products  14.8 us (14%)
  other arithmetic  13.1 us (13%)
  starting transfers between devices  9.78 us (9%)
  blocking collectives  8.02 us (8%)
  between operations  1.58 us (2%)
    ppermute x5, waiting for transfers between devices, extended(): lax.ppermute(tail, axis, [(i, (i + 1) % count) for i in range(count)])  15.5 us
    dot_general x27, matrix products, convolve(): jnp.dot(mixing, stacked, preferred_element_type=jnp.float32)  14.8 us
    ppermute x3, waiting for transfers between devices, shards(): lax.ppermute(ring[-1], 'gx', [(dev, (dev + 1) % 4) for dev in range(4)])  12.4 us
    all_to_all x1, blocking collectives, shards(): lax.all_to_all(coarse, 'gy', split_axis=3, concat_axis=2, tiled=True)  8.02 us
    ppermute x5, waiting for transfers between devices, extended(): lax.ppermute(head, axis, [((i + 1) % count, i) for i in range(count)])  7.78 us
    concatenate x18, local copies, waits for them, and re-layouts, convolve(): jnp.concatenate([padded[:, offset_x:offset_x + extent_x, offset_y:offset_...  6.73 us
    ppermute x5, starting transfers between devices, extended(): lax.ppermute(head, axis, [((i + 1) % count, i) for i in range(count)])  5.43 us
    reduce_sum x2, other arithmetic, average_pool(): return blocks.mean(axis=(2, 4, 6)).astype(jnp.bfloat16)  5.15 us
  transfers between devices with their start and end apart: 13, of which 13 were waited for; matrix products, arithmetic and copies ran while one was open for 3% of the time, Pallas kernels for 0%

profile of v1, /device:TPU:0, one launch (start us, length us, event | category | flops | bytes accessed | tf_op | source)
XLA Modules:
  0.0 104.1 jit_solution(6483933977915420068)
XLA Ops:
  0.6 1.5 %copy.174 = bf16[32,8,8,128]{3,0,2,1:T(8,128)(2,1)S(1)} copy(bf16[32,8,8,128]{3,2,1,0:T(8,128)(2,1)} %param.7) | data formatting | bytes 1048576 | tf_op args[0]
  2.1 3.0 %collective-permute-start = (bf16[32,1,8,128]{3,0,2,1:T(8,128)(2,1)S(1)}, bf16[32,1,8,128]{3,0,2,1:T(8,128)(2,1)S(1)}, u32[]{:S(2)}, u32[]{:S(2)}) collective-permute-start(bf16[32,1,8,128]{3,0,2,1:T(8,128)(2,1)S(1)} %get-tuple-element.57), channel_id=1, source_target_pairs={{0,8},{8,16},{16,24},{24,0},{1,9},{9,17},{17,25},{25,1},{2,10},{10... | collective-permute-start | bytes 196616 | tf_op jit(solution)/shard_map/ppermute | solution.py:14
  6.2 2.3 %collective-permute-done = bf16[32,1,8,128]{3,0,2,1:T(8,128)(2,1)S(1)} collective-permute-done((bf16[32,1,8,128]{3,0,2,1:T(8,128)(2,1)S(1)}, bf16[32,1,8,128]{3,0,2,1:T(8,128)(2,1)S(1)}, u32[]{:S(2)}, u32[]{:S(2)}) %collective-permute-start) | collective-permute-done | bytes 65568 | tf_op jit(solution)/shard_map/ppermute | solution.py:14
  9.9 2.2 %collective-permute-start.3 = (bf16[32,10,1,128]{3,0,2,1:T(8,128)(2,1)S(1)}, bf16[32,10,1,128]{3,0,2,1:T(8,128)(2,1)S(1)}, u32[]{:S(2)}, u32[]{:S(2)}) collective-permute-start(bf16[32,10,1,128]{3,0,2,1:T(8,128)(2,1)S(1)} %get-tuple-element.52), channel_id=1, source_target_pairs={{1,0},{2,1},{3,2},{4,3},{5,4},{6,5},{7,6},{0,7},{9,8},{10,9},{11,1... | collective-permute-start | bytes 245768 | tf_op jit(solution)/shard_map/ppermute | solution.py:16
  14.2 3.6 %collective-permute-done.2 = bf16[32,10,1,128]{3,0,2,1:T(8,128)(2,1)S(1)} collective-permute-done((bf16[32,10,1,128]{3,0,2,1:T(8,128)(2,1)S(1)}, bf16[32,10,1,128]{3,0,2,1:T(8,128)(2,1)S(1)}, u32[]{:S(2)}, u32[]{:S(2)}) %collective-permute-start.2) | collective-permute-done | bytes 81952 | tf_op jit(solution)/shard_map/ppermute | solution.py:14
  18.2 1.7 %maximum_maximum_fusion = (bf16[32,10,10,129]{3,0,2,1:T(8,128)(2,1)S(1)}, bf16[32,10,10,129]{3,0,2,1:T(8,128)(2,1)S(1)}) fusion(bf16[32,10,1,128]{3,0,2,1:T(8,128)(2,1)S(1)} %collective-permute-done.3, bf16[32,10,8,128]{3,0,2,1:T(8,128)(2,1)S(1)} %constant_dynamic-update-slice_fusion, bf16[32,10,1,128]{3,0,2,1:T(8,128)(2,1)S(1)} %collective-permute-done.2, ...), kind=kLoop, calls=%fused_computation.11 | loop fusion | flops 6604800 | bytes 2483200 | tf_op jit(solution)/shard_map/concatenate | solution.py:26
  19.9 2.8 %fusion.54 = (bf16[32,8,8,128]{3,0,2,1:T(8,128)(2,1)S(1)}, bf16[32,8,8,128]{3,0,2,1:T(8,128)(2,1)S(1)}, bf16[32,8,8,128]{3,0,2,1:T(8,128)(2,1)S(1)}, bf16[32,8,8...) fusion(bf16[32,10,10,129]{3,0,2,1:T(8,128)(2,1)S(1)} %get-tuple, ...), kind=kLoop, calls=%fused_computation.167 | loop fusion | bytes 18874368 | tf_op jit(solution)/shard_map/slice | solution.py:40
  31.1 1.1 %convolution_add_fusion.7 = f32[8192,32]{0,1:T(8,128)S(1)} fusion(f32[8192,32]{0,1:T(8,128)S(1)} %fusion.18, bf16[32,96]{1,0:T(8,128)(2,1)S(1)} %reshape.191, bf16[12,8,64,128]{3,2,1,0:T(8,128)(2,1)S(1)} %bitcast.227), kind=kOutput, calls=%fused_computation.9 | convolution fusion | flops 50593792 | bytes 3676160 | tf_op jit(solution)/shard_map/dot_general | solution.py:56
  33.4 1.1 %convolution_add_fusion.5 = f32[8192,32]{0,1:T(8,128)S(1)} fusion(f32[8192,32]{0,1:T(8,128)S(1)} %convolution_add_fusion.6, bf16[32,96]{1,0:T(8,128)(2,1)S(1)} %reshape.195, bf16[12,8,64,128]{3,2,1,0:T(8,128)(2,1)S(1)} %bitcast.230), kind=kOutput, calls=%fused_computation.7 | convolution fusion | flops 50593792 | bytes 3676160 | tf_op jit(solution)/shard_map/dot_general | solution.py:56
  36.7 1.1 %convolution_add_fusion.2 = f32[8192,32]{0,1:T(8,128)S(1)} fusion(f32[8192,32]{0,1:T(8,128)S(1)} %convolution_add_fusion.3, bf16[32,96]{1,0:T(8,128)(2,1)S(1)} %reshape.201, bf16[12,8,64,128]{3,2,1,0:T(8,128)(2,1)S(1)} %bitcast.233), kind=kOutput, calls=%fused_computation.4 | convolution fusion | flops 50593792 | bytes 3676160 | tf_op jit(solution)/shard_map/dot_general | solution.py:56
  37.9 1.1 %convolution_add_fusion.1 = f32[8192,32]{0,1:T(8,128)S(1)} fusion(f32[8192,32]{0,1:T(8,128)S(1)} %convolution_add_fusion.2, bf16[32,96]{1,0:T(8,128)(2,1)S(1)} %reshape.203, bf16[12,8,64,128]{3,2,1,0:T(8,128)(2,1)S(1)} %bitcast.232), kind=kOutput, calls=%fused_computation.3 | convolution fusion | flops 50593792 | bytes 3676160 | tf_op jit(solution)/shard_map/dot_general | solution.py:56
  39.0 1.1 %fusion.31 = bf16[32,8192]{1,0:T(8,128)(2,1)S(1)} fusion(f32[8192,32]{0,1:T(8,128)S(1)} %convolution_add_fusion.1, bf16[32,96]{1,0:T(8,128)(2,1)S(1)} %reshape.205, bf16[12,8,64,128]{3,2,1,0:T(8,128)(2,1)S(1)} %bitcast.234, f32[32]{0:T(128)S(1)} %copy-done.6), kind=kOutput, calls=%fused_computation.49 | convolution fusion | flops 51904512 | bytes 3152000 | tf_op jit(solution)/shard_map/dot_general | solution.py:56
  40.1 2.4 %copy.198 = f32[32,8192]{0,1:T(8,128)} copy(bf16[32,8192]{1,0:T(8,128)(2,1)S(1)} %fusion.31) | data formatting | bytes 1572864 | tf_op jit(solution)/shard_map/convert_element_type | solution.py:64
  42.5 4.8 %reduce_sum.18 = f32[32,4,4,64]{0,3,2,1:T(8,128)S(1)} reduce(f32[32,4,2,4,2,64,2]{0,6,5,4,3,2,1:T(2,128)} %bitcast.225, f32[]{:T(128)} %constant.36.clone.1), dimensions={2,4,6}, to_apply=%region_0.1 | reduce | flops 229376 | bytes 1179652 | tf_op jit(solution)/shard_map/reduce_sum | solution.py:67
  47.4 2.1 %collective-permute-start.5 = (bf16[32,1,4,64]{0,3,2,1:T(8,128)(2,1)S(1)}, bf16[32,1,4,64]{0,3,2,1:T(8,128)(2,1)S(1)}, u32[]{:S(2)}, u32[]{:S(2)}) collective-permute-start(bf16[32,1,4,64]{0,3,2,1:T(8,128)(2,1)S(1)} %get-tuple-element.101), channel_id=1, source_target_pairs={{8,0},{16,8},{24,16},{0,24},{9,1},{17,9},{25,17},{1,25},{10,2},{18... | collective-permute-start | bytes 49160 | tf_op jit(solution)/shard_map/ppermute | solution.py:16
  49.6 2.2 %collective-permute-done.5 = bf16[32,1,4,64]{0,3,2,1:T(8,128)(2,1)S(1)} collective-permute-done((bf16[32,1,4,64]{0,3,2,1:T(8,128)(2,1)S(1)}, bf16[32,1,4,64]{0,3,2,1:T(8,128)(2,1)S(1)}, u32[]{:S(2)}, u32[]{:S(2)}) %collective-permute-start.5) | collective-permute-done | bytes 16416 | tf_op jit(solution)/shard_map/ppermute | solution.py:16
  51.8 2.9 %collective-permute-done.4 = bf16[32,1,4,64]{0,3,2,1:T(8,128)(2,1)S(1)} collective-permute-done((bf16[32,1,4,64]{0,3,2,1:T(8,128)(2,1)S(1)}, bf16[32,1,4,64]{0,3,2,1:T(8,128)(2,1)S(1)}, u32[]{:S(2)}, u32[]{:S(2)}) %collective-permute-start.4) | collective-permute-done | bytes 16416 | tf_op jit(solution)/shard_map/ppermute | solution.py:14
  55.3 2.5 %collective-permute-done.7 = bf16[32,6,1,64]{0,3,2,1:T(8,128)(2,1)S(1)} collective-permute-done((bf16[32,6,1,64]{0,3,2,1:T(8,128)(2,1)S(1)}, bf16[32,6,1,64]{0,3,2,1:T(8,128)(2,1)S(1)}, u32[]{:S(2)}, u32[]{:S(2)}) %collective-permute-start.7) | collective-permute-done | bytes 24608 | tf_op jit(solution)/shard_map/ppermute | solution.py:16
  57.8 2.9 %collective-permute-done.6 = bf16[32,6,1,64]{0,3,2,1:T(8,128)(2,1)S(1)} collective-permute-done((bf16[32,6,1,64]{0,3,2,1:T(8,128)(2,1)S(1)}, bf16[32,6,1,64]{0,3,2,1:T(8,128)(2,1)S(1)}, u32[]{:S(2)}, u32[]{:S(2)}) %collective-permute-start.6) | collective-permute-done | bytes 24608 | tf_op jit(solution)/shard_map/ppermute | solution.py:14
  67.9 8.0 %all_to_all.18 = bf16[8,2,512]{2,1,0:T(2,128)(2,1)S(1)} all-to-all(bf16[8,2,512]{2,1,0:T(2,128)(2,1)S(1)} %reshape.247), channel_id=1, replica_groups=mesh['gx'=4,'gy'=8] {'gy'}, dimensions={0} | all-to-all | bytes 32768 | tf_op jit(solution)/shard_map/all_to_all | solution.py:77
  76.2 4.7 %collective-permute-done.8 = bf16[64,2,16,4]{0,2,3,1:T(8,128)(2,1)S(1)} collective-permute-done((bf16[64,2,16,4]{0,2,3,1:T(8,128)(2,1)S(1)}, bf16[64,2,16,4]{0,2,3,1:T(8,128)(2,1)S(1)}, u32[]{:S(2)}, u32[]{:S(2)}) %collective-permute-start.8) | collective-permute-done | bytes 16416 | tf_op jit(solution)/shard_map/ppermute | solution.py:80
  80.9 4.8 %collective-permute-done.9 = bf16[64,2,16,4]{0,2,3,1:T(8,128)(2,1)S(1)} collective-permute-done((bf16[64,2,16,4]{0,2,3,1:T(8,128)(2,1)S(1)}, bf16[64,2,16,4]{0,2,3,1:T(8,128)(2,1)S(1)}, u32[]{:S(2)}, u32[]{:S(2)}) %collective-permute-start.9) | collective-permute-done | bytes 16416 | tf_op jit(solution)/shard_map/ppermute | solution.py:80
  87.6 2.9 %collective-permute-done.10 = bf16[64,2,16,4]{0,2,3,1:T(8,128)(2,1)S(1)} collective-permute-done((bf16[64,2,16,4]{0,2,3,1:T(8,128)(2,1)S(1)}, bf16[64,2,16,4]{0,2,3,1:T(8,128)(2,1)S(1)}, u32[]{:S(2)}, u32[]{:S(2)}) %collective-permute-start.10) | collective-permute-done | bytes 16416 | tf_op jit(solution)/shard_map/ppermute | solution.py:80
  92.3 3.9 %collective-permute-done.11 = bf16[64,8,16,1]{0,2,3,1:T(8,128)(2,1)S(1)} collective-permute-done((bf16[64,8,16,1]{0,2,3,1:T(8,128)(2,1)S(1)}, bf16[64,8,16,1]{0,2,3,1:T(8,128)(2,1)S(1)}, u32[]{:S(2)}, u32[]{:S(2)}) %collective-permute-start.11) | collective-permute-done | bytes 16416 | tf_op jit(solution)/shard_map/ppermute | solution.py:14
  (165 shorter events, 35.8 us)
Async XLA Ops:
  0.6 7.8 %copy-start = (bf16[32,8,8,128]{3,2,1,0:T(8,128)(2,1)S(1)}, bf16[32,8,8,128]{3,2,1,0:T(8,128)(2,1)}, u32[]{:S(2)}) copy-start(bf16[32,8,8,128]{3,2,1,0:T(8,128)(2,1)} %param.7) | copy-start | bytes 1572868
  0.6 11.5 %copy-start.2 = (bf16[27,32,32]{2,1,0:T(8,128)(2,1)S(1)}, bf16[27,32,32]{2,1,0:T(8,128)(2,1)}, u32[]{:S(2)}) copy-start(bf16[27,32,32]{2,1,0:T(8,128)(2,1)} %param.8) | copy-start | bytes 165892
  2.1 6.3 %collective-permute-start = (bf16[32,1,8,128]{3,0,2,1:T(8,128)(2,1)S(1)}, bf16[32,1,8,128]{3,0,2,1:T(8,128)(2,1)S(1)}, u32[]{:S(2)}, u32[]{:S(2)}) collective-permute-start(bf16[32,1,8,128]{3,0,2,1:T(8,128)(2,1)S(1)} %get-tuple-element.57), channel_id=1, source_target_pairs={{0,8},{8,16},{16,24},{24,0},{1,9},{9,17},{17,25},{25,1},{2,10},{10... | collective-permute-start | bytes 196616 | tf_op jit(solution)/shard_map/ppermute | solution.py:14
  5.1 4.7 %collective-permute-start.1 = (bf16[32,1,8,128]{3,0,2,1:T(8,128)(2,1)S(1)}, bf16[32,1,8,128]{3,0,2,1:T(8,128)(2,1)S(1)}, u32[]{:S(2)}, u32[]{:S(2)}) collective-permute-start(bf16[32,1,8,128]{3,0,2,1:T(8,128)(2,1)S(1)} %get-tuple-element.56), channel_id=1, source_target_pairs={{8,0},{16,8},{24,16},{0,24},{9,1},{17,9},{25,17},{1,25},{10,2},{18... | collective-permute-start | bytes 196616 | tf_op jit(solution)/shard_map/ppermute | solution.py:16
  9.9 4.3 %collective-permute-start.3 = (bf16[32,10,1,128]{3,0,2,1:T(8,128)(2,1)S(1)}, bf16[32,10,1,128]{3,0,2,1:T(8,128)(2,1)S(1)}, u32[]{:S(2)}, u32[]{:S(2)}) collective-permute-start(bf16[32,10,1,128]{3,0,2,1:T(8,128)(2,1)S(1)} %get-tuple-element.52), channel_id=1, source_target_pairs={{1,0},{2,1},{3,2},{4,3},{5,4},{6,5},{7,6},{0,7},{9,8},{10,9},{11,1... | collective-permute-start | bytes 245768 | tf_op jit(solution)/shard_map/ppermute | solution.py:16
  12.1 5.7 %collective-permute-start.2 = (bf16[32,10,1,128]{3,0,2,1:T(8,128)(2,1)S(1)}, bf16[32,10,1,128]{3,0,2,1:T(8,128)(2,1)S(1)}, u32[]{:S(2)}, u32[]{:S(2)}) collective-permute-start(bf16[32,10,1,128]{3,0,2,1:T(8,128)(2,1)S(1)} %get-tuple-element.51), channel_id=1, source_target_pairs={{0,1},{1,2},{2,3},{3,4},{4,5},{5,6},{6,7},{7,0},{8,9},{9,10},{10,1... | collective-permute-start | bytes 245768 | tf_op jit(solution)/shard_map/ppermute | solution.py:14
  37.8 1.1 %copy-start.6 = (f32[32]{0:T(128)S(1)}, f32[32]{0:T(128)}, u32[]{:S(2)}) copy-start(f32[32]{0:T(128)} %param.9) | copy-start | bytes 388
  47.4 7.9 %copy-start.3 = (bf16[27,64,32]{1,2,0:T(8,128)(2,1)S(1)}, bf16[27,64,32]{1,2,0:T(8,128)(2,1)}, u32[]{:S(2)}) copy-start(bf16[27,64,32]{1,2,0:T(8,128)(2,1)} %param.10) | copy-start | bytes 331780
  47.4 4.4 %collective-permute-start.5 = (bf16[32,1,4,64]{0,3,2,1:T(8,128)(2,1)S(1)}, bf16[32,1,4,64]{0,3,2,1:T(8,128)(2,1)S(1)}, u32[]{:S(2)}, u32[]{:S(2)}) collective-permute-start(bf16[32,1,4,64]{0,3,2,1:T(8,128)(2,1)S(1)} %get-tuple-element.101), channel_id=1, source_target_pairs={{8,0},{16,8},{24,16},{0,24},{9,1},{17,9},{25,17},{1,25},{10,2},{18... | collective-permute-start | bytes 49160 | tf_op jit(solution)/shard_map/ppermute | solution.py:16
  49.5 5.2 %collective-permute-start.4 = (bf16[32,1,4,64]{0,3,2,1:T(8,128)(2,1)S(1)}, bf16[32,1,4,64]{0,3,2,1:T(8,128)(2,1)S(1)}, u32[]{:S(2)}, u32[]{:S(2)}) collective-permute-start(bf16[32,1,4,64]{0,3,2,1:T(8,128)(2,1)S(1)} %get-tuple-element.100), channel_id=1, source_target_pairs={{0,8},{8,16},{16,24},{24,0},{1,9},{9,17},{17,25},{25,1},{2,10},{10... | collective-permute-start | bytes 49160 | tf_op jit(solution)/shard_map/ppermute | solution.py:14
  54.7 3.1 %collective-permute-start.7 = (bf16[32,6,1,64]{0,3,2,1:T(8,128)(2,1)S(1)}, bf16[32,6,1,64]{0,3,2,1:T(8,128)(2,1)S(1)}, u32[]{:S(2)}, u32[]{:S(2)}) collective-permute-start(bf16[32,6,1,64]{0,3,2,1:T(8,128)(2,1)S(1)} %get-tuple-element.76), channel_id=1, source_target_pairs={{1,0},{2,1},{3,2},{4,3},{5,4},{6,5},{7,6},{0,7},{9,8},{10,9},{11,1... | collective-permute-start | bytes 73736 | tf_op jit(solution)/shard_map/ppermute | solution.py:16
  54.8 5.9 %collective-permute-start.6 = (bf16[32,6,1,64]{0,3,2,1:T(8,128)(2,1)S(1)}, bf16[32,6,1,64]{0,3,2,1:T(8,128)(2,1)S(1)}, u32[]{:S(2)}, u32[]{:S(2)}) collective-permute-start(bf16[32,6,1,64]{0,3,2,1:T(8,128)(2,1)S(1)} %get-tuple-element.75), channel_id=1, source_target_pairs={{0,1},{1,2},{2,3},{3,4},{4,5},{5,6},{6,7},{7,0},{8,9},{9,10},{10,1... | collective-permute-start | bytes 73736 | tf_op jit(solution)/shard_map/ppermute | solution.py:14
  66.2 0.8 copy-start.4
  66.7 19.0 %copy-start.1 = (bf16[27,128,64]{1,2,0:T(8,128)(2,1)S(1)}, bf16[27,128,64]{1,2,0:T(8,128)(2,1)}, u32[]{:S(2)}) copy-start(bf16[27,128,64]{1,2,0:T(8,128)(2,1)} %param.12) | copy-start | bytes 1327108
  76.0 4.9 %collective-permute-start.8 = (bf16[64,2,16,4]{0,2,3,1:T(8,128)(2,1)S(1)}, bf16[64,2,16,4]{0,2,3,1:T(8,128)(2,1)S(1)}, u32[]{:S(2)}, u32[]{:S(2)}) collective-permute-start(bf16[64,2,16,4]{0,2,3,1:T(8,128)(2,1)S(1)} %bitcast.247), channel_id=1, source_target_pairs={{0,8},{8,16},{16,24},{24,0},{1,9},{9,17},{17,25},{25,1},{2,10},{10... | collective-permute-start | bytes 49160 | tf_op jit(solution)/shard_map/ppermute | solution.py:80
  80.9 4.8 %collective-permute-start.9 = (bf16[64,2,16,4]{0,2,3,1:T(8,128)(2,1)S(1)}, bf16[64,2,16,4]{0,2,3,1:T(8,128)(2,1)S(1)}, u32[]{:S(2)}, u32[]{:S(2)}) collective-permute-start(bf16[64,2,16,4]{0,2,3,1:T(8,128)(2,1)S(1)} %collective-permute-done.8), channel_id=1, source_target_pairs={{0,8},{8,16},{16,24},{24,0},{1,9},{9,17},{17,25},{25,1},{2,10},{10... | collective-permute-start | bytes 49160 | tf_op jit(solution)/shard_map/ppermute | solution.py:80
  85.7 4.8 %collective-permute-start.10 = (bf16[64,2,16,4]{0,2,3,1:T(8,128)(2,1)S(1)}, bf16[64,2,16,4]{0,2,3,1:T(8,128)(2,1)S(1)}, u32[]{:S(2)}, u32[]{:S(2)}) collective-permute-start(bf16[64,2,16,4]{0,2,3,1:T(8,128)(2,1)S(1)} %collective-permute-done.9), channel_id=1, source_target_pairs={{0,8},{8,16},{16,24},{24,0},{1,9},{9,17},{17,25},{25,1},{2,10},{10... | collective-permute-start | bytes 49160 | tf_op jit(solution)/shard_map/ppermute | solution.py:80
  90.7 1.7 %collective-permute-start.12 = (bf16[64,8,16,1]{0,2,3,1:T(8,128)(2,1)S(1)}, bf16[64,8,16,1]{0,2,3,1:T(8,128)(2,1)S(1)}, u32[]{:S(2)}, u32[]{:S(2)}) collective-permute-start(bf16[64,8,16,1]{0,2,3,1:T(8,128)(2,1)S(1)} %get-tuple-element.96), channel_id=1, source_target_pairs={{1,0},{2,1},{3,2},{4,3},{5,4},{6,5},{7,6},{0,7},{9,8},{10,9},{11,1... | collective-permute-start | bytes 49160 | tf_op jit(solution)/shard_map/ppermute | solution.py:16
  90.7 5.5 %collective-permute-start.11 = (bf16[64,8,16,1]{0,2,3,1:T(8,128)(2,1)S(1)}, bf16[64,8,16,1]{0,2,3,1:T(8,128)(2,1)S(1)}, u32[]{:S(2)}, u32[]{:S(2)}) collective-permute-start(bf16[64,8,16,1]{0,2,3,1:T(8,128)(2,1)S(1)} %get-tuple-element.95), channel_id=1, source_target_pairs={{0,1},{1,2},{2,3},{3,4},{4,5},{5,6},{6,7},{7,0},{8,9},{9,10},{10,1... | collective-permute-start | bytes 49160 | tf_op jit(solution)/shard_map/ppermute | solution.py:14
  102.3 0.9 copy-start.5
